TPU v7x, 32 devices: a whole 2x2x4 slice. The times are simulated.
32 devices in a mesh: ctx: 8 (over y, x, core), tp: 4 (over z).
Axes of the slice: x: 2, y: 2, z: 4, core: 2. Of those that a mesh axis runs over, the one named last changes fastest.
Arguments:
- hidden_in: bfloat16 [2048, 4096], P(('ctx', 'tp')), may hold values from -6 to 6
- norm_gain: float32 [4096], replicated, may hold values from 0.5 to 1.5
- proj_weight: bfloat16 [4096, 4096], P(None, 'tp'), may hold values from -0.09375 to 0.09375
- conv_in: bfloat16 [2048, 4096], P('ctx', 'tp'), may hold values from -6 to 6
- conv_weight: float32 [4, 4096], P(None, 'tp'), may hold values from -3 to 3
- conv_bias: float32 [4096], P('tp'), may hold values from -3 to 3
- act_grad: bfloat16 [2048, 4096], P('ctx', 'tp'), may hold values from -6 to 6
Outputs:
- hidden_input_gradient: bfloat16 [2048, 4096], P(('ctx', 'tp'))
- norm_gain_gradient: float32 [4096], replicated
- taps_grad: float32 [4, 4096], P(None, 'tp')
- bias_grad: float32 [4096], P('tp')
All inputs are finite; a program needn't handle non-finite values.
Results may differ from a plain program's by a relative error of at most 0.013.
Values may be sent and summed in bfloat16 or wider, within the bound.
No kernel may reach another device: no remote copies, remote signals or barrier semaphores. Data moves between devices by JAX's collectives and lax.ppermute only.
A program may use at most 64 MiB of HBM per device.

v0:
```python
import jax
import jax.numpy as jnp
from jax import lax
from jax.sharding import PartitionSpec as P


def from_behind(block, axis, distance):
    devices = range(lax.axis_size(axis))
    route = [(i - distance, i) for i in devices if i - distance in devices]
    return lax.ppermute(block, axis, route)


def preact_of(padded, taps, offset, count_tok):
    tap_count = taps.shape[0]
    return offset[None, :] + sum(
        (
            taps[index][None, :] * padded[tap_count - 1 - index : tap_count - 1 - index + count_tok]
            for index in range(tap_count)
        )
    )


def grad_of(preact, cotangent):
    sigmoid_v = jax.nn.sigmoid(preact)
    return cotangent.astype(jnp.float32) * sigmoid_v * (1.0 + preact * (1.0 - sigmoid_v))


def on_device(hidden_in, norm_gain, proj_weight, conv_in, conv_weight, conv_bias, act_grad):
    count_tok = conv_in.shape[0]
    tap_count = conv_weight.shape[0]
    edge_rows = tap_count - 1
    earlier = from_behind(conv_in[count_tok - edge_rows :], "ctx", 1)
    later_in, later_grad = from_behind((conv_in[:edge_rows], act_grad[:edge_rows]), "ctx", -1)
    padded = jnp.concatenate([earlier, conv_in], 0).astype(jnp.float32)
    preact = preact_of(padded, conv_weight, conv_bias, count_tok)
    pre_grad = grad_of(preact, act_grad)
    tail_pad = jnp.concatenate([conv_in[count_tok - edge_rows :], later_in], 0).astype(jnp.float32)
    tail_pre = preact_of(tail_pad, conv_weight, conv_bias, edge_rows)
    next_grad = grad_of(tail_pre, later_grad)
    taps_part = jnp.stack(
        [
            jnp.sum(pre_grad * padded[edge_rows - index : edge_rows - index + count_tok], 0)
            for index in range(tap_count)
        ],
        0,
    )
    bias_part = jnp.sum(pre_grad, 0)
    taps_grad, bias_grad = lax.psum((taps_part, bias_part), "ctx")
    after = jnp.concatenate([pre_grad, next_grad], 0)
    in_grad = sum(
        (
            conv_weight[index][None, :] * after[index : index + count_tok]
            for index in range(tap_count)
        )
    ).astype(jnp.bfloat16)
    whole_term = lax.dot_general(
        in_grad, proj_weight, (((1,), (1,)), ((), ())), preferred_element_type=jnp.float32
    )
    normalized_gradient = lax.psum_scatter(
        whole_term.astype(jnp.bfloat16), "tp", scatter_dimension=0, tiled=True
    ).astype(jnp.float32)
    hidden_state = hidden_in.astype(jnp.float32)
    root_mean_square = jnp.sqrt(jnp.mean(hidden_state * hidden_state, -1, keepdims=True) + 1e-05)
    normalized_input = hidden_state / root_mean_square
    norm_gain_gradient = lax.psum(jnp.sum(normalized_gradient * normalized_input, 0), ("ctx", "tp"))
    scaled_gradient = norm_gain[None, :] * normalized_gradient
    mean_correction = jnp.mean(scaled_gradient * normalized_input, -1, keepdims=True)
    hidden_input_gradient = (
        (scaled_gradient - normalized_input * mean_correction) / root_mean_square
    ).astype(jnp.bfloat16)
    return (hidden_input_gradient, norm_gain_gradient, taps_grad, bias_grad)


def solution(mesh):
    return jax.shard_map(
        on_device,
        mesh=mesh,
        in_specs=(
            P(("ctx", "tp"), None),
            P(),
            P(None, "tp"),
            P("ctx", "tp"),
            P(None, "tp"),
            P("tp"),
            P("ctx", "tp"),
        ),
        out_specs=(P(("ctx", "tp"), None), P(), P(None, "tp"), P("tp")),
        check_vma=False,
    )
```

profile of v0, /device:TPU:0, one launch (start us, length us, event | category | flops | bytes accessed | tf_op | source)
XLA Modules:
  0.0 122.8 jit_solution(8762573390390648197)
XLA Ops:
  7.2 0.0 copy-start.2
  7.2 0.0 copy-start.4
  7.2 0.0 reduce-scatter.2.cloned.1.call-start
  7.2 0.8 fusion.26
  8.0 2.4 %collective-permute-start = (bf16[3,1024]{1,0:T(4,128)(2,1)S(1)}, bf16[3,1024]{1,0:T(4,128)(2,1)S(1)}, u32[]{:S(2)}, u32[]{:S(2)}) collective-permute-start(bf16[3,1024]{1,0:T(4,128)(2,1)S(1)} %get-tuple-element.14), channel_id=1, source_target_pairs={{0,4},{4,8},{8,12},{12,16},{16,20},{20,24},{24,28},{1,5},{5,9},{9,... | collective-permute-start | bytes 18440 | tf_op jit(solution)/shard_map/ppermute | solution.py:10
  10.4 1.3 %collective-permute-start.2 = (bf16[3,1024]{1,0:T(4,128)(2,1)S(1)}, bf16[3,1024]{1,0:T(4,128)(2,1)S(1)}, u32[]{:S(2)}, u32[]{:S(2)}) collective-permute-start(bf16[3,1024]{1,0:T(4,128)(2,1)S(1)} %get-tuple-element.15), channel_id=1, source_target_pairs={{4,0},{8,4},{12,8},{16,12},{20,16},{24,20},{28,24},{5,1},{9,5},{13... | collective-permute-start | bytes 18440 | tf_op jit(solution)/shard_map/ppermute | solution.py:10
  11.7 0.7 slice.76
  12.5 1.3 %collective-permute-start.1 = (bf16[3,1024]{1,0:T(4,128)(2,1)S(1)}, bf16[3,1024]{1,0:T(4,128)(2,1)S(1)}, u32[]{:S(2)}, u32[]{:S(2)}) collective-permute-start(bf16[3,1024]{1,0:T(4,128)(2,1)S(1)} %slice.76), channel_id=1, source_target_pairs={{4,0},{8,4},{12,8},{16,12},{20,16},{24,20},{28,24},{5,1},{9,5},{13... | collective-permute-start | bytes 18440 | tf_op jit(solution)/shard_map/ppermute | solution.py:10
  13.7 0.9 fusion.27
  14.6 0.0 collective-permute-done
  14.6 1.2 maximum_convert_fusion
  15.8 0.0 copy-done.2
  15.8 0.0 copy-done.4
  15.9 1.3 %multiply_reduce_fusion.3 = (f32[1024]{0:T(1024)S(1)}, f32[1024]{0:T(1024)S(1)}, f32[1024]{0:T(1024)S(1)}, f32[1024]{0:T(1024)S(1)}, f32[1024]{0:T(1024)S(1)}, /*index=5*/f32[256,1024]{1,0:T(8,128)S(1)}) fusion(f32[259,1024]{1,0:T(8,128)S(1)} %maximum_convert_fusion, f32[1024]{0:T(1024)S(1)} %bitcast.15, f32[1024]{0:T(1024)S(1)} %bitcast.18, ...), kind=kLoop, calls=%fused_computation.27 | loop fusion | flops 6810624 | bytes 5808128 | tf_op jit(solution)/shard_map/reduce_sum | solution.py:42
  17.1 0.0 collective-permute-done.2
  17.2 1.1 collective-permute-done.1
  18.3 7.4 %convolution_convert_fusion = bf16[256,4096]{1,0:T(8,128)(2,1)} fusion(bf16[4096,1024]{1,0:T(8,128)(2,1)} %param.9, f32[3,1024]{1,0:T(4,128)S(1)} %add_multiply_fusion.1, f32[256,1024]{1,0:T(8,128)S(1)} %get-tuple-element.13, f32[1024]{0:T(1024)S(1)} %bitcast.17, f32[1024]{0:T(1024)S(1)} %bitcast.20, f32[1024]{0:T(1024)S(1)} %bitcast.14, f32[1024]{0:T(1024)S(1)} %bitcast.11), kind=kOutput, calls=%fused_computation | convolution fusion | flops 2151415808 | bytes 11563008 | tf_op jit(solution)/shard_map/dot_general | solution.py:56
  25.6 0.0 copy-start
  25.6 0.0 copy-start.3
  25.6 0.0 reduce-scatter.2.cloned.1.call-update
  25.7 1.0 copy-done
  26.7 0.2 fusion.6
  26.9 29.4 %all-reduce = (f32[4,1024]{1,0:T(4,128)}, f32[1024]{0:T(1024)}) all-reduce(f32[4,1024]{1,0:T(4,128)S(1)} %pad_maximum_fusion.1, f32[1024]{0:T(1024)S(1)} %get-tuple-element.10), channel_id=1, replica_groups=mesh['ctx'=8,'tp'=4] {'ctx'}, use_global_device_ids=true, to_apply=%region_9.0 | all-reduce | flops 5120 | bytes 40960 | tf_op jit(solution)/shard_map/psum | solution.py:48
  56.4 17.4 %reduce-scatter.2.cloned.1.call-done = bf16[64,4096]{1,0:T(8,128)(2,1)} async-done(((bf16[256,4096]{1,0:T(8,128)(2,1)}), bf16[64,4096]{1,0:T(8,128)(2,1)}) %reduce-scatter.2.cloned.1.call-update) | async-done | bytes 524304 | tf_op jit(solution)/shard_map/reduce_scatter | solution.py:59
  73.7 0.0 copy-done.3
  73.7 0.0 copy-start.1
  73.7 1.6 %fusion.5 = (f32[4096]{0:T(1024)S(1)}, f32[64]{0:T(128)S(1)}) fusion(bf16[64,4096]{1,0:T(8,128)(2,1)} %reduce-scatter.2.cloned.1.call-done, f32[64]{0:T(128)S(1)} %add_sqrt_fusion, bf16[64,4096]{1,0:T(8,128)(2,1)S(1)} %copy-done, f32[4096]{0:T(1024)S(1)} %copy-done.3), kind=kLoop, calls=%fused_computation.12 | loop fusion | flops 2092992 | bytes 1081856 | tf_op jit(solution)/shard_map/reduce_sum | solution.py:65
  75.3 39.5 %psum.21 = f32[4096]{0:T(1024)} all-reduce(f32[4096]{0:T(1024)S(1)} %get-tuple-element.8), channel_id=1, replica_groups=mesh['ctx'=8,'tp'=4] {'ctx','tp'}, use_global_device_ids=true, to_apply=%region_4.0 | all-reduce | flops 4096 | bytes 32768 | tf_op jit(solution)/shard_map/psum | solution.py:65
  114.8 0.0 copy-done.1
  114.8 1.1 fusion.4
  (5 shorter events, 0.1 us)
Async XLA Ops:
  7.2 8.7 %copy-start.2 = (bf16[256,1024]{1,0:T(8,128)(2,1)S(1)}, bf16[256,1024]{1,0:T(8,128)(2,1)}, u32[]{:S(2)}) copy-start(bf16[256,1024]{1,0:T(8,128)(2,1)} %param.13) | copy-start | bytes 1572868
  7.2 8.7 %copy-start.4 = (f32[1024]{0:T(1024)S(1)}, f32[1024]{0:T(1024)}, u32[]{:S(2)}) copy-start(f32[1024]{0:T(1024)} %param.12) | copy-start | bytes 12292
  7.2 66.6 %reduce-scatter.2.cloned.1.call-start = ((), (), s32[]{:S(2)}) async-start(), calls=%async_computation.1 | async-start | bytes 2621440 | tf_op jit(solution)/shard_map/reduce_scatter | solution.py:59
  8.0 6.6 %collective-permute-start = (bf16[3,1024]{1,0:T(4,128)(2,1)S(1)}, bf16[3,1024]{1,0:T(4,128)(2,1)S(1)}, u32[]{:S(2)}, u32[]{:S(2)}) collective-permute-start(bf16[3,1024]{1,0:T(4,128)(2,1)S(1)} %get-tuple-element.14), channel_id=1, source_target_pairs={{0,4},{4,8},{8,12},{12,16},{16,20},{20,24},{24,28},{1,5},{5,9},{9,... | collective-permute-start | bytes 18440 | tf_op jit(solution)/shard_map/ppermute | solution.py:10
  10.4 6.7 %collective-permute-start.2 = (bf16[3,1024]{1,0:T(4,128)(2,1)S(1)}, bf16[3,1024]{1,0:T(4,128)(2,1)S(1)}, u32[]{:S(2)}, u32[]{:S(2)}) collective-permute-start(bf16[3,1024]{1,0:T(4,128)(2,1)S(1)} %get-tuple-element.15), channel_id=1, source_target_pairs={{4,0},{8,4},{12,8},{16,12},{20,16},{24,20},{28,24},{5,1},{9,5},{13... | collective-permute-start | bytes 18440 | tf_op jit(solution)/shard_map/ppermute | solution.py:10
  12.5 5.8 %collective-permute-start.1 = (bf16[3,1024]{1,0:T(4,128)(2,1)S(1)}, bf16[3,1024]{1,0:T(4,128)(2,1)S(1)}, u32[]{:S(2)}, u32[]{:S(2)}) collective-permute-start(bf16[3,1024]{1,0:T(4,128)(2,1)S(1)} %slice.76), channel_id=1, source_target_pairs={{4,0},{8,4},{12,8},{16,12},{20,16},{24,20},{28,24},{5,1},{9,5},{13... | collective-permute-start | bytes 18440 | tf_op jit(solution)/shard_map/ppermute | solution.py:10
  25.6 1.0 copy-start
  25.6 48.1 %copy-start.3 = (f32[4096]{0:T(1024)S(1)}, f32[4096]{0:T(1024)}, u32[]{:S(2)}) copy-start(f32[4096]{0:T(1024)} %param.8) | copy-start | bytes 49156
  73.7 41.1 %copy-start.1 = (bf16[64,4096]{1,0:T(8,128)(2,1)S(1)}, bf16[64,4096]{1,0:T(8,128)(2,1)}, u32[]{:S(2)}) copy-start(bf16[64,4096]{1,0:T(8,128)(2,1)} %reduce-scatter.2.cloned.1.call-done) | copy-start | bytes 1572868
Sparse Core Ops, SparseCore 0:
  25.8 47.9 reduce-scatter.1
where the time goes:
time: 123 us
  blocking collectives  68.9 us (56%)
  waiting for transfers between devices  18.5 us (15%)
  between operations  14.1 us (11%)
  matrix products  7.36 us (6%)
  other arithmetic  5.41 us (4%)
  starting transfers between devices  5.01 us (4%)
  local copies, waits for them, and re-layouts  3.44 us (3%)
    psum x1, blocking collectives, on_device(): lax.psum(jnp.sum(normalized_gradient * normalized_input, 0), ('ctx', 'tp'))  39.5 us
    psum x1, blocking collectives, on_device(): taps_grad, bias_grad = lax.psum((taps_part, bias_part), 'ctx')  29.4 us
    reduce_scatter x1, waiting for transfers between devices, on_device(): lax.psum_scatter(whole_term.astype(jnp.bfloat16), 'tp', scatter_dimension...  17.4 us
    dot_general x1, matrix products, on_device(): lax.dot_general(in_grad, proj_weight, (((1,), (1,)), ((), ())), preferred...  7.36 us
    ppermute x3, starting transfers between devices, from_behind(): return lax.ppermute(block, axis, route)  4.97 us
  transfers between devices with their start and end apart: 4, of which 2 were waited for; matrix products, arithmetic and copies ran while one was open for 4% of the time, Pallas kernels for 0%

commit v1 on v0

--- a/solution.py
+++ b/solution.py
@@ -62,7 +62,9 @@
     hidden_state = hidden_in.astype(jnp.float32)
     root_mean_square = jnp.sqrt(jnp.mean(hidden_state * hidden_state, -1, keepdims=True) + 1e-05)
     normalized_input = hidden_state / root_mean_square
-    norm_gain_gradient = lax.psum(jnp.sum(normalized_gradient * normalized_input, 0), ("ctx", "tp"))
+    block_2 = jnp.sum(normalized_gradient * normalized_input, 0)
+    parts = lax.all_gather(block_2, ("ctx", "tp"), axis=0, tiled=False)
+    norm_gain_gradient = parts.sum(axis=0)
     scaled_gradient = norm_gain[None, :] * normalized_gradient
     mean_correction = jnp.mean(scaled_gradient * normalized_input, -1, keepdims=True)
     hidden_input_gradient = (

time: 123 us -> 155 us (1.26)
  blocking collectives: 68.9 us -> 99.8 us
    all_gather x0 -> x1, blocking collectives: none -> 70.4 us  [on_device(): parts = lax.all_gather(block_2, ('ctx', 'tp'), axis=0, tiled=False)]
    psum x1 -> x0, blocking collectives: 39.5 us -> none  [on_device(): lax.psum(jnp.sum(normalized_gradient * normalized_input, 0), ('ctx', 'tp'))]
  transfers between devices with their start and end apart: 4 -> 4, of which waited for: 2 -> 2; matrix products, arithmetic and copies ran while one was open for 4% -> 3% of each run, Pallas kernels for 0% -> 0%
where the time goes in v1:
time: 155 us; the launch traced here: 154 us
  blocking collectives  99.8 us (64%)
  waiting for transfers between devices  18.5 us (12%)
  between operations  14.2 us (9%)
  matrix products  7.36 us (5%)
  other arithmetic  6 us (4%)
  starting transfers between devices  5.01 us (3%)
  local copies, waits for them, and re-layouts  3.53 us (2%)
    all_gather x1, blocking collectives, on_device(): parts = lax.all_gather(block_2, ('ctx', 'tp'), axis=0, tiled=False)  70.4 us
    psum x1, blocking collectives, on_device(): taps_grad, bias_grad = lax.psum((taps_part, bias_part), 'ctx')  29.4 us
    reduce_scatter x1, waiting for transfers between devices, on_device(): lax.psum_scatter(whole_term.astype(jnp.bfloat16), 'tp', scatter_dimension...  17.4 us
    dot_general x1, matrix products, on_device(): lax.dot_general(in_grad, proj_weight, (((1,), (1,)), ((), ())), preferred...  7.36 us
    ppermute x3, starting transfers between devices, from_behind(): return lax.ppermute(block, axis, route)  4.97 us
  transfers between devices with their start and end apart: 4, of which 2 were waited for; matrix products, arithmetic and copies ran while one was open for 3% of the time, Pallas kernels for 0%

profile of v1, /device:TPU:0, one launch (start us, length us, event | category | flops | bytes accessed | tf_op | source)
XLA Modules:
  0.0 154.4 jit_solution(7776847725076292415)
XLA Ops:
  7.2 0.0 copy-start.2
  7.2 0.0 copy-start.4
  7.2 0.0 reduce-scatter.2.cloned.1.call-start
  7.2 0.8 fusion.26
  8.0 2.4 %collective-permute-start = (bf16[3,1024]{1,0:T(4,128)(2,1)S(1)}, bf16[3,1024]{1,0:T(4,128)(2,1)S(1)}, u32[]{:S(2)}, u32[]{:S(2)}) collective-permute-start(bf16[3,1024]{1,0:T(4,128)(2,1)S(1)} %get-tuple-element.14), channel_id=1, source_target_pairs={{0,4},{4,8},{8,12},{12,16},{16,20},{20,24},{24,28},{1,5},{5,9},{9,... | collective-permute-start | bytes 18440 | tf_op jit(solution)/shard_map/ppermute | solution.py:10
  10.4 1.3 collective-permute-start.2
  11.7 0.7 slice.76
  12.5 1.3 collective-permute-start.1
  13.7 0.9 fusion.27
  14.6 0.0 collective-permute-done
  14.6 1.2 maximum_convert_fusion
  15.8 0.0 copy-done.2
  15.8 0.0 copy-done.4
  15.9 1.3 multiply_reduce_fusion.3
  17.1 0.0 collective-permute-done.2
  17.2 1.1 collective-permute-done.1
  18.3 7.4 %convolution_convert_fusion = bf16[256,4096]{1,0:T(8,128)(2,1)} fusion(bf16[4096,1024]{1,0:T(8,128)(2,1)} %param.9, f32[3,1024]{1,0:T(4,128)S(1)} %add_multiply_fusion.1, f32[256,1024]{1,0:T(8,128)S(1)} %get-tuple-element.13, f32[1024]{0:T(1024)S(1)} %bitcast.17, f32[1024]{0:T(1024)S(1)} %bitcast.20, f32[1024]{0:T(1024)S(1)} %bitcast.14, f32[1024]{0:T(1024)S(1)} %bitcast.11), kind=kOutput, calls=%fused_computation | convolution fusion | flops 2151415808 | bytes 11563008 | tf_op jit(solution)/shard_map/dot_general | solution.py:56
  25.6 0.0 copy-start
  25.6 0.0 copy-start.3
  25.6 0.0 reduce-scatter.2.cloned.1.call-update
  25.7 1.0 copy-done
  26.7 0.2 fusion.6
  26.9 29.4 %all-reduce = (f32[4,1024]{1,0:T(4,128)}, f32[1024]{0:T(1024)}) all-reduce(f32[4,1024]{1,0:T(4,128)S(1)} %pad_maximum_fusion.1, f32[1024]{0:T(1024)S(1)} %get-tuple-element.10), channel_id=1, replica_groups=mesh['ctx'=8,'tp'=4] {'ctx'}, use_global_device_ids=true, to_apply=%region_9.0 | all-reduce | flops 5120 | bytes 40960 | tf_op jit(solution)/shard_map/psum | solution.py:48
  56.4 17.4 %reduce-scatter.2.cloned.1.call-done = bf16[64,4096]{1,0:T(8,128)(2,1)} async-done(((bf16[256,4096]{1,0:T(8,128)(2,1)}), bf16[64,4096]{1,0:T(8,128)(2,1)}) %reduce-scatter.2.cloned.1.call-update) | async-done | bytes 524304 | tf_op jit(solution)/shard_map/reduce_scatter | solution.py:59
  73.7 0.0 copy-done.3
  73.7 1.5 fusion.5
  75.2 0.0 copy-start.1
  75.3 70.4 %all-gather = f32[131072]{0:T(1024)S(1)} all-gather(f32[4096]{0:T(1024)S(1)} %get-tuple-element.8), channel_id=2, replica_groups=mesh['ctx'=8,'tp'=4] {'ctx','tp'}, dimensions={0}, use_global_device_ids=true | all-gather | bytes 540672 | tf_op jit(solution)/shard_map/all_gather | solution.py:66
  145.7 0.1 reshape.22
  145.8 0.7 reduce_sum.84
  146.5 0.0 copy-done.1
  146.5 1.1 fusion.4
  (5 shorter events, 0.1 us)
Async XLA Ops:
  7.2 8.7 %copy-start.2 = (bf16[256,1024]{1,0:T(8,128)(2,1)S(1)}, bf16[256,1024]{1,0:T(8,128)(2,1)}, u32[]{:S(2)}) copy-start(bf16[256,1024]{1,0:T(8,128)(2,1)} %param.13) | copy-start | bytes 1572868
  7.2 8.7 %copy-start.4 = (f32[1024]{0:T(1024)S(1)}, f32[1024]{0:T(1024)}, u32[]{:S(2)}) copy-start(f32[1024]{0:T(1024)} %param.12) | copy-start | bytes 12292
  7.2 66.6 %reduce-scatter.2.cloned.1.call-start = ((), (), s32[]{:S(2)}) async-start(), calls=%async_computation.1 | async-start | bytes 2621440 | tf_op jit(solution)/shard_map/reduce_scatter | solution.py:59
  8.0 6.6 %collective-permute-start = (bf16[3,1024]{1,0:T(4,128)(2,1)S(1)}, bf16[3,1024]{1,0:T(4,128)(2,1)S(1)}, u32[]{:S(2)}, u32[]{:S(2)}) collective-permute-start(bf16[3,1024]{1,0:T(4,128)(2,1)S(1)} %get-tuple-element.14), channel_id=1, source_target_pairs={{0,4},{4,8},{8,12},{12,16},{16,20},{20,24},{24,28},{1,5},{5,9},{9,... | collective-permute-start | bytes 18440 | tf_op jit(solution)/shard_map/ppermute | solution.py:10
  10.4 6.7 %collective-permute-start.2 = (bf16[3,1024]{1,0:T(4,128)(2,1)S(1)}, bf16[3,1024]{1,0:T(4,128)(2,1)S(1)}, u32[]{:S(2)}, u32[]{:S(2)}) collective-permute-start(bf16[3,1024]{1,0:T(4,128)(2,1)S(1)} %get-tuple-element.15), channel_id=1, source_target_pairs={{4,0},{8,4},{12,8},{16,12},{20,16},{24,20},{28,24},{5,1},{9,5},{13... | collective-permute-start | bytes 18440 | tf_op jit(solution)/shard_map/ppermute | solution.py:10
  12.5 5.8 %collective-permute-start.1 = (bf16[3,1024]{1,0:T(4,128)(2,1)S(1)}, bf16[3,1024]{1,0:T(4,128)(2,1)S(1)}, u32[]{:S(2)}, u32[]{:S(2)}) collective-permute-start(bf16[3,1024]{1,0:T(4,128)(2,1)S(1)} %slice.76), channel_id=1, source_target_pairs={{4,0},{8,4},{12,8},{16,12},{20,16},{24,20},{28,24},{5,1},{9,5},{13... | collective-permute-start | bytes 18440 | tf_op jit(solution)/shard_map/ppermute | solution.py:10
  25.6 1.0 copy-start
  25.6 48.1 %copy-start.3 = (f32[4096]{0:T(1024)S(1)}, f32[4096]{0:T(1024)}, u32[]{:S(2)}) copy-start(f32[4096]{0:T(1024)} %param.8) | copy-start | bytes 49156
  75.2 71.2 %copy-start.1 = (bf16[64,4096]{1,0:T(8,128)(2,1)S(1)}, bf16[64,4096]{1,0:T(8,128)(2,1)}, u32[]{:S(2)}) copy-start(bf16[64,4096]{1,0:T(8,128)(2,1)} %reduce-scatter.2.cloned.1.call-done) | copy-start | bytes 1572868
Sparse Core Ops, SparseCore 0:
  25.8 47.9 reduce-scatter.1
